TPU v7x, 32 devices: a whole 2x2x4 slice. The times are simulated.
32 devices in a mesh: groups: 2 (over y), wide: 4 (over z), narrow: 4 (over x, core).
Axes of the slice: x: 2, y: 2, z: 4, core: 2. Of those that a mesh axis runs over, the one named last changes fastest.
Arguments:
- cont_queries: bfloat16 [32, 128, 64, 128], P(('groups', 'wide'), None, 'narrow'), parts along dimension 0, may hold values from -5 to 5
- cont_keys: bfloat16 [32, 128, 8, 128], P(('groups', 'wide'), None, 'narrow'), parts along dimension 0, may hold values from -5 to 5
- cont_values: bfloat16 [32, 128, 8, 128], P(('groups', 'wide'), None, 'narrow'), parts along dimension 0, may hold values from -5 to 5
- prefix_kv: bfloat16 [8, 2, 128, 8, 128], P(('groups', 'wide'), None, None, 'narrow'), parts along dimension 0, may hold values from -5 to 5
- probe: bfloat16 [64, 128], P('narrow'), may hold values from -0.5 to 0.5
- question_row: int32 [8], P('groups'), parts along dimension 0, may hold values from 0 to 3, each once
- cont_slot: int32 [32], P(('groups', 'wide')), parts along dimension 0, may hold values from 0 to 15, each once
- cont_length: int32 [32], P(('groups', 'wide')), parts along dimension 0, may hold values from 1 to 128
- gold: int32 [8], P('groups'), parts along dimension 0, may hold values from 0 to 3
Outputs:
- token_score: float32 [32, 128], P(('groups', 'wide')), parts along dimension 0
- owned_logprob: float32 [8, 4], P(('groups', 'wide')), parts along dimension 0
- owned_loss: float32 [8], P(('groups', 'wide')), parts along dimension 0
There are 2 independent parts, one for each index of `groups`. A program takes and returns all parts, laid end to end along the dimension named above; an argument that names none is the same for every part. Nothing has to cross between parts.
All inputs are finite; a program needn't handle non-finite values.
Results may differ from a plain program's by a relative error of at most 0.0065.
Values may be sent and summed in bfloat16 or wider, within the bound.
No kernel may reach another device: no remote copies, remote signals or barrier semaphores. Data moves between devices by JAX's collectives and lax.ppermute only.
A program may use at most 64 MiB of HBM per device.

v0:
```python
import jax
import jax.numpy as jnp
from jax import lax
from jax.sharding import PartitionSpec as P

ANSWERS = 4


def attend_part(queries, keys, values, allowed, scale_factor):
    scores = (
        jnp.einsum("ctkgd,cjkd->ckgtj", queries, keys, preferred_element_type=jnp.float32)
        * scale_factor
    )
    scores = jnp.where(allowed[None, None, None, :, :], scores, -jnp.inf)
    row_max = jnp.max(scores, axis=-1)
    expo = jnp.exp(scores - row_max[..., None])
    total = jnp.sum(expo, axis=-1)
    weights = expo.astype(jnp.bfloat16)
    summed = jnp.einsum("ckgtj,cjkd->ctkgd", weights, values, preferred_element_type=jnp.float32)
    return (row_max, total, summed)


def to_rows(stat):
    return jnp.transpose(stat, (0, 3, 1, 2))[..., None]


def per_device(
    cont_queries,
    cont_keys,
    cont_values,
    prefix_kv,
    probe,
    question_row,
    cont_slot,
    cont_length,
    gold,
):
    cont_count, clen, heads_here, head_dim = cont_queries.shape
    kv_here = cont_keys.shape[2]
    group_size = heads_here // kv_here
    quest_here = prefix_kv.shape[0]
    pref_len = prefix_kv.shape[2]
    questions = question_row.shape[0]
    scale_factor = 1.0 / head_dim**0.5
    wanted = question_row[cont_slot // ANSWERS]
    piece = lax.all_gather(prefix_kv, "wide", axis=0, tiled=True)
    count = piece.shape[0]
    hits = (wanted[:, None] == jnp.arange(count, dtype=jnp.int32)[None, :]).astype(jnp.bfloat16)
    chosen = jnp.einsum("cn,nkpvd->ckpvd", hits, piece, preferred_element_type=jnp.float32)
    mine = chosen.astype(jnp.bfloat16)
    queries = cont_queries.reshape(cont_count, clen, kv_here, group_size, head_dim)
    causal = jnp.arange(clen)[:, None] >= jnp.arange(clen)[None, :]
    keys_all = jnp.concatenate([mine[:, 0], cont_keys], axis=1)
    values_all = jnp.concatenate([mine[:, 1], cont_values], axis=1)
    allowed = jnp.concatenate([jnp.ones((clen, pref_len), dtype=bool), causal], axis=1)
    row_max, total, summed = attend_part(queries, keys_all, values_all, allowed, scale_factor)
    output = summed / to_rows(total)
    attended = output.astype(jnp.bfloat16).reshape(cont_count, clen, heads_here, head_dim)
    partial_value = jnp.einsum("cthd,hd->ct", attended, probe, preferred_element_type=jnp.float32)
    token_score = lax.psum(partial_value, "narrow")
    valid = jnp.arange(clen)[None, :] < cont_length[:, None]
    choice_score = jnp.sum(jnp.where(valid, token_score, 0.0), axis=1)
    target = wanted * ANSWERS + cont_slot % ANSWERS
    spots = target[:, None] == jnp.arange(questions * ANSWERS, dtype=jnp.int32)[None, :]
    term = jnp.sum(jnp.where(spots, choice_score[:, None], 0.0), axis=0).reshape(questions, ANSWERS)
    first_row = lax.axis_index("wide") * quest_here
    totals = lax.psum(term, "wide")
    owned = lax.dynamic_slice_in_dim(totals, first_row, quest_here, 0)
    logprob = owned - jax.nn.logsumexp(owned, axis=1, keepdims=True)
    owned_rows = first_row + jnp.arange(quest_here, dtype=jnp.int32)
    matches = question_row[None, :] == owned_rows[:, None]
    gold_owned = jnp.sum(jnp.where(matches, gold[None, :], 0), axis=1)
    answer_ids = jnp.arange(ANSWERS, dtype=jnp.int32)[None, :]
    owned_loss = -jnp.sum(jnp.where(answer_ids == gold_owned[:, None], logprob, 0.0), axis=1)
    return (token_score, logprob, owned_loss)


def solution(mesh):
    return jax.shard_map(
        per_device,
        mesh=mesh,
        in_specs=(
            P(("groups", "wide"), None, "narrow", None),
            P(("groups", "wide"), None, "narrow", None),
            P(("groups", "wide"), None, "narrow", None),
            P(("groups", "wide"), None, None, "narrow", None),
            P("narrow", None),
            P("groups"),
            P(("groups", "wide")),
            P(("groups", "wide")),
            P("groups"),
        ),
        out_specs=(P(("groups", "wide"), None), P(("groups", "wide"), None), P(("groups", "wide"))),
        check_vma=False,
    )
```

profile of v0, /device:TPU:0, one launch (start us, length us, event | category | flops | bytes accessed | tf_op | source)
XLA Modules:
  0.0 57.5 jit_solution(3568872146050696365)
XLA Ops:
  0.6 0.0 copy-start
  0.6 0.8 %compare_select_fusion = s32[4]{0:T(128)S(1)} fusion(s32[4]{0:T(128)} %param.15), kind=kLoop, calls=%fused_computation.27 | loop fusion | flops 72 | bytes 32 | tf_op jit(solution)/shard_map/select_n | solution.py:45
  1.5 1.3 %gather_fusion = s32[4]{0:T(128)S(1)} fusion(s32[4]{0:T(128)} %param.14, s32[1024]{0:T(1024)S(1)} %pad_clamp_fusion), kind=kCustom, calls=%fused_computation | custom fusion | bytes 48 | tf_op jit(solution)/shard_map/gather | solution.py:45
  2.8 0.9 %copy.34 = bf16[1,2,128,2,128]{4,2,3,1,0:T(8,128)(2,1)S(1)} copy(bf16[1,2,128,2,128]{4,3,2,1,0:T(2,128)(2,1)} %param.12) | data formatting | bytes 262144 | tf_op args[3]
  3.7 17.4 %all_gather.3 = bf16[4,2,128,2,128]{4,2,3,1,0:T(8,128)(2,1)S(1)} all-gather(bf16[1,2,128,2,128]{4,2,3,1,0:T(8,128)(2,1)S(1)} %copy.34), channel_id=1, replica_groups=mesh['groups'=2,'wide'=4,'narrow'=4] {'wide'}, dimensions={0}, use_global_device_ids=true | all-gather | bytes 655360 | tf_op jit(solution)/shard_map/all_gather | solution.py:46
  21.1 0.5 convolution_convert_fusion
  21.6 0.2 slice_bitcast_fusion.1
  21.8 1.3 %copy.36 = bf16[4,128,2,128]{3,0,2,1:T(4,128)(2,1)S(1)} copy(bf16[4,128,2,128]{3,2,1,0:T(2,128)(2,1)} %param.11) | data formatting | bytes 524288 | tf_op args[2]
  23.1 1.3 %copy.37 = bf16[4,128,2,128]{3,0,2,1:T(4,128)(2,1)S(1)} copy(bf16[4,128,2,128]{3,2,1,0:T(2,128)(2,1)} %param.10) | data formatting | bytes 524288 | tf_op args[1]
  24.4 0.7 %maximum_bitcast_fusion = (bf16[4,256,2,128,1]{3,0,2,1,4:T(4,128)(2,1)S(1)}, bf16[4,256,2,128,1]{3,0,2,1,4:T(4,128)(2,1)S(1)}) fusion(bf16[4,128,2,128]{3,0,2,1:T(4,128)(2,1)S(1)} %copy.36, bf16[4,128,2,128]{3,0,2,1:T(4,128)(2,1)S(1)} %get-tuple-element.5, bf16[4,128,2,128]{3,0,2,1:T(4,128)(2,1)S(1)} %copy.37, bf16[4,128,2,128]{3,0,2,1:T(4,128)(2,1)S(1)} %get-tuple-element.6), kind=kLoop, calls=%fused_computation.16 | loop fusion | flops 524288 | bytes 2097152 | tf_op jit(solution)/shard_map/concatenate | solution.py:54
  25.1 0.0 copy-done
  25.1 1.5 %fusion.2 = (f32[4,2,8,128]{3,2,1,0:T(8,128)S(1)}, f32[4,2,256,128,8]{3,2,4,1,0:T(8,128)S(1)}) fusion(pred[128,256]{0,1:T(8,128)(4,1)S(1)} %concatenate.10, bf16[4,128,2,8,128]{4,3,2,1,0:T(8,128)(2,1)S(1)} %bitcast.41, bf16[4,256,2,128,1]{3,0,2,1,4:T(4,128)(2,1)S(1)} %get-tuple-element.10), kind=kOutput, calls=%fused_computation.5 | convolution fusion | flops 543154176 | bytes 11075584 | tf_op jit(solution)/shard_map/ctkgd,cjkd->ckgtj/dot_general | solution.py:11
  26.7 2.2 %fusion = f32[4,2,8,128]{3,2,1,0:T(8,128)S(1)} fusion(f32[4,2,256,128,8]{3,2,4,1,0:T(8,128)S(1)} %get-tuple-element.8, f32[4,2,8,128]{3,2,1,0:T(8,128)S(1)} %get-tuple-element.7, pred[128,256]{0,1:T(8,128)(4,1)S(1)} %concatenate.10), kind=kLoop, calls=%fused_computation.3 | loop fusion | flops 8380416 | bytes 8486912 | tf_op jit(solution)/shard_map/reduce_sum | solution.py:17
  28.9 0.0 copy-start.2
  28.9 0.0 copy-start.4
  28.9 0.0 copy-start.6
  29.0 0.0 copy-start.1
  29.0 0.0 copy-start.5
  29.0 2.4 %fusion.5 = bf16[4,128,2,8,128]{1,4,3,2,0:T(8,128)(2,1)S(1)} fusion(f32[4,128,2,8]{1,3,2,0:T(8,128)S(1)} %bitcast.43, f32[4,2,256,128,8]{3,2,4,1,0:T(8,128)S(1)} %get-tuple-element.8, f32[4,2,8,128]{3,2,1,0:T(8,128)S(1)} %get-tuple-element.7, pred[128,256]{0,1:T(8,128)(4,1)S(1)} %concatenate.10, bf16[4,256,2,128,1]{3,0,2,1,4:T(4,128)(2,1)S(1)} %get-tuple-element.9), kind=kOutput, calls=%fused_computation.8 | convolution fusion | flops 547356672 | bytes 11108352 | tf_op jit(solution)/shard_map/ckgtj,cjkd->ctkgd/dot_general | solution.py:19
  31.3 0.0 copy-done.2
  31.3 0.4 fusion.17
  31.7 5.6 %psum.14 = f32[4,128]{1,0:T(4,128)S(1)} all-reduce(f32[4,128]{1,0:T(4,128)S(1)} %bitcast.45), channel_id=1, replica_groups=mesh['groups'=2,'wide'=4,'narrow'=4] {'narrow'}, use_global_device_ids=true, to_apply=%region_2.3 | all-reduce | flops 512 | bytes 4096 | tf_op jit(solution)/shard_map/psum | solution.py:60
  37.4 0.0 copy-done.4
  37.4 0.2 select_reduce_fusion.1
  37.6 0.0 copy-done.6
  37.6 0.1 select_reduce_fusion
  37.7 0.1 reshape.54
  37.7 12.5 %psum.15 = f32[4,4]{1,0:T(4,128)S(1)} all-reduce(f32[4,4]{1,0:T(4,128)S(1)} %reshape.54), channel_id=1, replica_groups=mesh['groups'=2,'wide'=4,'narrow'=4] {'wide'}, use_global_device_ids=true, to_apply=%region_5.6 | all-reduce | flops 16 | bytes 128 | tf_op jit(solution)/shard_map/psum | solution.py:67
  50.2 0.6 %fusion.27 = f32[]{:T(128)} fusion(f32[4,4]{1,0:T(4,128)S(1)} %psum.15, s32[]{:T(128)S(6)} %select_n.48), kind=kLoop, calls=%fused_computation.50 | loop fusion | flops 3 | bytes 24 | tf_op jit(solution)/shard_map/reduce_max | solution.py:69
  52.1 0.6 %exponential_reduce_fusion = f32[]{:T(128)} fusion(f32[]{:T(128)} %bitcast.15, f32[4,4]{1,0:T(4,128)S(1)} %psum.15, s32[]{:T(128)S(6)} %select_n.48), kind=kLoop, calls=%fused_computation.45 | loop fusion | flops 7 | bytes 28 | tf_op jit(solution)/shard_map/reduce_sum | solution.py:69
  53.4 0.6 %fusion.23 = s32[]{:T(128)} fusion(s32[4]{0:T(128)S(1)} %copy-done.5, s32[4]{0:T(128)S(1)} %copy-done.1, s32[]{:T(128)S(6)} %axis_index.15), kind=kLoop, calls=%fused_computation.43 | loop fusion | flops 11 | bytes 40 | tf_op jit(solution)/shard_map/reduce_sum | solution.py:72
  54.1 1.8 %fusion.24 = (f32[]{:T(128)}, f32[1,4]{1,0:T(1,128)}) fusion(s32[]{:T(128)} %fusion.23, f32[]{:T(128)} %bitcast.17, f32[4,4]{1,0:T(4,128)S(1)} %psum.15, s32[]{:T(128)S(6)} %select_n.48), kind=kLoop, calls=%fused_computation.44 | loop fusion | flops 15 | bytes 48 | tf_op jit(solution)/shard_map/reduce_sum | solution.py:74
  (8 shorter events, 0.1 us)
Async XLA Ops:
  0.6 24.5 %copy-start = (bf16[4,128,16,128]{3,2,1,0:T(8,128)(2,1)S(1)}, bf16[4,128,16,128]{3,2,1,0:T(8,128)(2,1)}, u32[]{:S(2)}) copy-start(bf16[4,128,16,128]{3,2,1,0:T(8,128)(2,1)} %param.9) | copy-start | bytes 6291460
  28.9 2.4 %copy-start.2 = (bf16[16,128]{1,0:T(8,128)(2,1)S(1)}, bf16[16,128]{1,0:T(8,128)(2,1)}, u32[]{:S(2)}) copy-start(bf16[16,128]{1,0:T(8,128)(2,1)} %param.13) | copy-start | bytes 12292
  28.9 8.4 %copy-start.4 = (s32[4]{0:T(128)S(1)}, s32[4]{0:T(128)}, u32[]{:S(2)}) copy-start(s32[4]{0:T(128)} %param.16) | copy-start | bytes 52
  28.9 8.6 %copy-start.6 = (s32[4]{0:T(128)S(1)}, s32[4]{0:T(128)}, u32[]{:S(2)}) copy-start(s32[4]{0:T(128)} %param.15) | copy-start | bytes 52
  29.0 24.5 %copy-start.1 = (s32[4]{0:T(128)S(1)}, s32[4]{0:T(128)}, u32[]{:S(2)}) copy-start(s32[4]{0:T(128)} %param.14) | copy-start | bytes 52
  29.0 24.5 %copy-start.5 = (s32[4]{0:T(128)S(1)}, s32[4]{0:T(128)}, u32[]{:S(2)}) copy-start(s32[4]{0:T(128)} %param.17) | copy-start | bytes 52
  37.4 19.0 %copy-start.3 = (f32[4,128]{1,0:T(4,128)}, f32[4,128]{1,0:T(4,128)S(1)}, u32[]{:S(2)}) copy-start(f32[4,128]{1,0:T(4,128)S(1)} %psum.14) | copy-start | bytes 6148
where the time goes:
time: 57.8 us; the launch traced here: 57.5 us
  blocking collectives  35.5 us (61%)
  other arithmetic  7.63 us (13%)
  local copies, waits for them, and re-layouts  5.13 us (9%)
  matrix products  4.82 us (8%)
  between operations  4.47 us (8%)
    all_gather x1, blocking collectives, per_device(): piece = lax.all_gather(prefix_kv, 'wide', axis=0, tiled=True)  17.4 us
    psum x1, blocking collectives, per_device(): totals = lax.psum(term, 'wide')  12.5 us
    psum x1, blocking collectives, per_device(): token_score = lax.psum(partial_value, 'narrow')  5.64 us
    unnamed x17, local copies, waits for them, and re-layouts  3.56 us
    dot_general x1, matrix products, attend_part(): jnp.einsum('ckgtj,cjkd->ctkgd', weights, values, preferred_element_type=j...  2.35 us
    reduce_sum x1, other arithmetic, attend_part(): total = jnp.sum(expo, axis=-1)  2.23 us
    reduce_sum x1, other arithmetic, per_device(): jnp.sum(jnp.where(answer_ids == gold_owned[:, None], logprob, 0.0), axis=1)  1.75 us
    dot_general x1, matrix products, attend_part(): jnp.einsum('ctkgd,cjkd->ckgtj', queries, keys, preferred_element_type=jnp...  1.54 us

commit v1 on v0

--- a/solution.py
+++ b/solution.py
@@ -1,9 +1,27 @@
+import functools
 import jax
 import jax.numpy as jnp
 from jax import lax
 from jax.sharding import PartitionSpec as P
 
 ANSWERS = 4
+
+
+def yards_match(in_array, mesh_name):
+    devs = lax.axis_size(mesh_name)
+
+    def assign_matrix(main, top):
+        if top >= devs:
+            return main
+        in_order = []
+        for w in range(devs):
+            in_order.append((w, w ^ top))
+        return assign_matrix(main + lax.ppermute(main, axis_name=mesh_name, perm=in_order), 2 * top)
+
+    return assign_matrix(in_array, 1)
+
+
+panels_report = functools.partial(yards_match, mesh_name="wide")
 
 
 def attend_part(queries, keys, values, allowed, scale_factor):
@@ -64,7 +82,7 @@
     spots = target[:, None] == jnp.arange(questions * ANSWERS, dtype=jnp.int32)[None, :]
     term = jnp.sum(jnp.where(spots, choice_score[:, None], 0.0), axis=0).reshape(questions, ANSWERS)
     first_row = lax.axis_index("wide") * quest_here
-    totals = lax.psum(term, "wide")
+    totals = panels_report(term)
     owned = lax.dynamic_slice_in_dim(totals, first_row, quest_here, 0)
     logprob = owned - jax.nn.logsumexp(owned, axis=1, keepdims=True)
     owned_rows = first_row + jnp.arange(quest_here, dtype=jnp.int32)

time: 57.8 us -> 53.7 us (0.929)
  blocking collectives: 35.5 us -> 23 us
  starting transfers between devices: 0 us -> 4.69 us
  waiting for transfers between devices: 0 us -> 2.86 us
  other arithmetic: 7.63 us -> 8.37 us
    psum x1 -> x0, blocking collectives: 12.5 us -> none  [per_device(): totals = lax.psum(term, 'wide')]
    ppermute x0 -> x2, starting transfers between devices: none -> 4.69 us  [assign_matrix(): lax.ppermute(main, axis_name=mesh_name, perm=in_order)]
    ppermute x0 -> x2, waiting for transfers between devices: none -> 2.86 us  [assign_matrix(): lax.ppermute(main, axis_name=mesh_name, perm=in_order)]
    add x1, other arithmetic: 0.01 us -> 0.67 us  [per_device(): target = wanted * ANSWERS + cont_slot % ANSWERS]
    unnamed x17 -> x15, local copies, waits for them, and re-layouts: 3.56 us -> 3.55 us
  transfers between devices with their start and end apart: 0 -> 2, of which waited for: 0 -> 2; matrix products, arithmetic and copies ran while one was open for 0% -> 1% of each run, Pallas kernels for 0% -> 0%
where the time goes in v1:
time: 53.7 us; the launch traced here: 53.4 us
  blocking collectives  23 us (43%)
  other arithmetic  8.37 us (16%)
  local copies, waits for them, and re-layouts  5.12 us (10%)
  matrix products  4.82 us (9%)
  starting transfers between devices  4.69 us (9%)
  between operations  4.49 us (8%)
  waiting for transfers between devices  2.86 us (5%)
    all_gather x1, blocking collectives, per_device(): piece = lax.all_gather(prefix_kv, 'wide', axis=0, tiled=True)  17.4 us
    psum x1, blocking collectives, per_device(): token_score = lax.psum(partial_value, 'narrow')  5.64 us
    ppermute x2, starting transfers between devices, assign_matrix(): lax.ppermute(main, axis_name=mesh_name, perm=in_order)  4.69 us
    unnamed x15, local copies, waits for them, and re-layouts  3.55 us
    ppermute x2, waiting for transfers between devices, assign_matrix(): lax.ppermute(main, axis_name=mesh_name, perm=in_order)  2.86 us
    dot_general x1, matrix products, attend_part(): jnp.einsum('ckgtj,cjkd->ctkgd', weights, values, preferred_element_type=j...  2.35 us
    reduce_sum x1, other arithmetic, attend_part(): total = jnp.sum(expo, axis=-1)  2.23 us
    reduce_sum x1, other arithmetic, per_device(): jnp.sum(jnp.where(answer_ids == gold_owned[:, None], logprob, 0.0), axis=1)  1.76 us
  transfers between devices with their start and end apart: 2, of which 2 were waited for; matrix products, arithmetic and copies ran while one was open for 1% of the time, Pallas kernels for 0%

profile of v1, /device:TPU:0, one launch (start us, length us, event | category | flops | bytes accessed | tf_op | source)
XLA Modules:
  0.0 53.4 jit_solution(4943295451239697367)
XLA Ops:
  0.6 0.0 copy-start
  0.7 0.8 %compare_select_fusion = s32[4]{0:T(128)S(1)} fusion(s32[4]{0:T(128)} %param.15), kind=kLoop, calls=%fused_computation.27 | loop fusion | flops 72 | bytes 32 | tf_op jit(solution)/shard_map/select_n | solution.py:63
  1.5 0.9 %copy.34 = bf16[1,2,128,2,128]{4,2,3,1,0:T(8,128)(2,1)S(1)} copy(bf16[1,2,128,2,128]{4,3,2,1,0:T(2,128)(2,1)} %param.12) | data formatting | bytes 262144 | tf_op args[3]
  2.4 17.4 %all_gather.3 = bf16[4,2,128,2,128]{4,2,3,1,0:T(8,128)(2,1)S(1)} all-gather(bf16[1,2,128,2,128]{4,2,3,1,0:T(8,128)(2,1)S(1)} %copy.34), channel_id=1, replica_groups=mesh['groups'=2,'wide'=4,'narrow'=4] {'wide'}, dimensions={0}, use_global_device_ids=true | all-gather | bytes 655360 | tf_op jit(solution)/shard_map/all_gather | solution.py:64
  19.8 1.3 %gather_fusion = s32[4]{0:T(128)S(1)} fusion(s32[4]{0:T(128)} %param.14, s32[1024]{0:T(1024)S(1)} %pad_clamp_fusion), kind=kCustom, calls=%fused_computation | custom fusion | bytes 48 | tf_op jit(solution)/shard_map/gather | solution.py:63
  21.1 0.7 %fusion.22 = s32[4]{0:T(128)S(1)} fusion(s32[4]{0:T(128)S(1)} %gather_fusion, s32[4]{0:T(128)} %param.15), kind=kLoop, calls=%fused_computation.42 | loop fusion | flops 52 | bytes 48 | tf_op jit(solution)/shard_map/add | solution.py:81
  21.7 0.5 %convolution_convert_fusion = bf16[4,2,128,2,128]{4,0,3,2,1:T(4,128)(2,1)S(1)} fusion(bf16[4,2,128,2,128]{4,2,3,1,0:T(8,128)(2,1)S(1)} %all_gather.3, s32[4]{0:T(128)S(1)} %gather_fusion), kind=kOutput, calls=%fused_computation.15 | convolution fusion | flops 2359312 | bytes 1048592 | tf_op jit(solution)/shard_map/cn,nkpvd->ckpvd/dot_general | solution.py:67
  22.3 0.2 slice_bitcast_fusion.1
  22.5 1.3 %copy.36 = bf16[4,128,2,128]{3,0,2,1:T(4,128)(2,1)S(1)} copy(bf16[4,128,2,128]{3,2,1,0:T(2,128)(2,1)} %param.11) | data formatting | bytes 524288 | tf_op args[2]
  23.8 1.3 %copy.37 = bf16[4,128,2,128]{3,0,2,1:T(4,128)(2,1)S(1)} copy(bf16[4,128,2,128]{3,2,1,0:T(2,128)(2,1)} %param.10) | data formatting | bytes 524288 | tf_op args[1]
  25.1 0.7 %maximum_bitcast_fusion = (bf16[4,256,2,128,1]{3,0,2,1,4:T(4,128)(2,1)S(1)}, bf16[4,256,2,128,1]{3,0,2,1,4:T(4,128)(2,1)S(1)}) fusion(bf16[4,128,2,128]{3,0,2,1:T(4,128)(2,1)S(1)} %copy.36, bf16[4,128,2,128]{3,0,2,1:T(4,128)(2,1)S(1)} %get-tuple-element.5, bf16[4,128,2,128]{3,0,2,1:T(4,128)(2,1)S(1)} %copy.37, bf16[4,128,2,128]{3,0,2,1:T(4,128)(2,1)S(1)} %get-tuple-element.6), kind=kLoop, calls=%fused_computation.16 | loop fusion | flops 524288 | bytes 2097152 | tf_op jit(solution)/shard_map/concatenate | solution.py:72
  25.8 1.5 %fusion.2 = (f32[4,2,8,128]{3,2,1,0:T(8,128)S(1)}, f32[4,2,256,128,8]{3,2,4,1,0:T(8,128)S(1)}) fusion(pred[128,256]{0,1:T(8,128)(4,1)S(1)} %concatenate.10, bf16[4,128,2,8,128]{4,3,2,1,0:T(8,128)(2,1)S(1)} %bitcast.41, bf16[4,256,2,128,1]{3,0,2,1,4:T(4,128)(2,1)S(1)} %get-tuple-element.10), kind=kOutput, calls=%fused_computation.5 | convolution fusion | flops 543154176 | bytes 11075584 | tf_op jit(solution)/shard_map/ctkgd,cjkd->ckgtj/dot_general | solution.py:29
  27.3 2.2 %fusion = f32[4,2,8,128]{3,2,1,0:T(8,128)S(1)} fusion(f32[4,2,256,128,8]{3,2,4,1,0:T(8,128)S(1)} %get-tuple-element.8, f32[4,2,8,128]{3,2,1,0:T(8,128)S(1)} %get-tuple-element.7, pred[128,256]{0,1:T(8,128)(4,1)S(1)} %concatenate.10), kind=kLoop, calls=%fused_computation.3 | loop fusion | flops 8380416 | bytes 8486912 | tf_op jit(solution)/shard_map/reduce_sum | solution.py:35
  29.6 0.0 copy-start.2
  29.6 0.0 copy-start.4
  29.6 0.0 copy-start.1
  29.6 0.0 copy-start.5
  29.6 2.4 %fusion.5 = bf16[4,128,2,8,128]{1,4,3,2,0:T(8,128)(2,1)S(1)} fusion(f32[4,128,2,8]{1,3,2,0:T(8,128)S(1)} %bitcast.43, f32[4,2,256,128,8]{3,2,4,1,0:T(8,128)S(1)} %get-tuple-element.8, f32[4,2,8,128]{3,2,1,0:T(8,128)S(1)} %get-tuple-element.7, pred[128,256]{0,1:T(8,128)(4,1)S(1)} %concatenate.10, bf16[4,256,2,128,1]{3,0,2,1,4:T(4,128)(2,1)S(1)} %get-tuple-element.9), kind=kOutput, calls=%fused_computation.8 | convolution fusion | flops 547356672 | bytes 11108352 | tf_op jit(solution)/shard_map/ckgtj,cjkd->ctkgd/dot_general | solution.py:37
  32.0 0.4 fusion.17
  32.4 5.6 %psum.7 = f32[4,128]{1,0:T(4,128)S(1)} all-reduce(f32[4,128]{1,0:T(4,128)S(1)} %bitcast.45), channel_id=1, replica_groups=mesh['groups'=2,'wide'=4,'narrow'=4] {'narrow'}, use_global_device_ids=true, to_apply=%region_2.3 | all-reduce | flops 512 | bytes 4096 | tf_op jit(solution)/shard_map/psum | solution.py:78
  38.0 0.2 select_reduce_fusion.1
  38.2 0.1 select_reduce_fusion
  38.3 0.1 reshape.54
  38.4 2.1 %collective-permute-start = (f32[4,4]{1,0:T(4,128)S(1)}, f32[4,4]{1,0:T(4,128)S(1)}, u32[]{:S(2)}, u32[]{:S(2)}) collective-permute-start(f32[4,4]{1,0:T(4,128)S(1)} %reshape.54), channel_id=1, source_target_pairs={{0,4},{4,0},{8,12},{12,8},{1,5},{5,1},{9,13},{13,9},{2,6},{6,2},{1... | collective-permute-start | bytes 200 | tf_op jit(solution)/shard_map/ppermute | solution.py:19
  40.5 0.0 copy-done.1
  40.5 0.6 %fusion.23 = s32[]{:T(128)} fusion(s32[4]{0:T(128)S(1)} %copy-done.5, s32[4]{0:T(128)S(1)} %copy-done.1, s32[]{:T(128)S(6)} %axis_index.15), kind=kLoop, calls=%fused_computation.43 | loop fusion | flops 11 | bytes 40 | tf_op jit(solution)/shard_map/reduce_sum | solution.py:90
  41.2 0.9 %collective-permute-done = f32[4,4]{1,0:T(4,128)S(1)} collective-permute-done((f32[4,4]{1,0:T(4,128)S(1)}, f32[4,4]{1,0:T(4,128)S(1)}, u32[]{:S(2)}, u32[]{:S(2)}) %collective-permute-start) | collective-permute-done | bytes 96 | tf_op jit(solution)/shard_map/ppermute | solution.py:19
  42.1 2.5 %collective-permute-start.1 = (f32[4,4]{1,0:T(4,128)S(1)}, f32[4,4]{1,0:T(4,128)S(1)}, u32[]{:S(2)}, u32[]{:S(2)}) collective-permute-start(f32[4,4]{1,0:T(4,128)S(1)} %add.30), channel_id=1, source_target_pairs={{0,8},{4,12},{8,0},{12,4},{1,9},{5,13},{9,1},{13,5},{2,10},{6,14},... | collective-permute-start | bytes 200 | tf_op jit(solution)/shard_map/ppermute | solution.py:19
  44.6 1.9 %collective-permute-done.1 = f32[4,4]{1,0:T(4,128)S(1)} collective-permute-done((f32[4,4]{1,0:T(4,128)S(1)}, f32[4,4]{1,0:T(4,128)S(1)}, u32[]{:S(2)}, u32[]{:S(2)}) %collective-permute-start.1) | collective-permute-done | bytes 96 | tf_op jit(solution)/shard_map/ppermute | solution.py:19
  46.6 0.6 %fusion.27 = f32[]{:T(128)} fusion(f32[4,4]{1,0:T(4,128)S(1)} %add.31, s32[]{:T(128)S(6)} %select_n.48), kind=kLoop, calls=%fused_computation.50 | loop fusion | flops 3 | bytes 24 | tf_op jit(solution)/shard_map/reduce_max | solution.py:87
  48.5 0.7 %exponential_reduce_fusion = f32[]{:T(128)} fusion(f32[]{:T(128)} %bitcast.15, f32[4,4]{1,0:T(4,128)S(1)} %add.31, s32[]{:T(128)S(6)} %select_n.48), kind=kLoop, calls=%fused_computation.45 | loop fusion | flops 7 | bytes 28 | tf_op jit(solution)/shard_map/reduce_sum | solution.py:87
  49.9 1.8 %fusion.24 = (f32[]{:T(128)}, f32[1,4]{1,0:T(1,128)}) fusion(s32[]{:T(128)} %fusion.23, f32[]{:T(128)} %bitcast.17, f32[4,4]{1,0:T(4,128)S(1)} %add.31, s32[]{:T(128)S(6)} %select_n.48), kind=kLoop, calls=%fused_computation.44 | loop fusion | flops 15 | bytes 48 | tf_op jit(solution)/shard_map/reduce_sum | solution.py:92
  (11 shorter events, 0.1 us)
Async XLA Ops:
  0.6 25.2 %copy-start = (bf16[4,128,16,128]{3,2,1,0:T(8,128)(2,1)S(1)}, bf16[4,128,16,128]{3,2,1,0:T(8,128)(2,1)}, u32[]{:S(2)}) copy-start(bf16[4,128,16,128]{3,2,1,0:T(8,128)(2,1)} %param.9) | copy-start | bytes 6291460
  29.6 2.4 %copy-start.2 = (bf16[16,128]{1,0:T(8,128)(2,1)S(1)}, bf16[16,128]{1,0:T(8,128)(2,1)}, u32[]{:S(2)}) copy-start(bf16[16,128]{1,0:T(8,128)(2,1)} %param.13) | copy-start | bytes 12292
  29.6 8.4 %copy-start.4 = (s32[4]{0:T(128)S(1)}, s32[4]{0:T(128)}, u32[]{:S(2)}) copy-start(s32[4]{0:T(128)} %param.16) | copy-start | bytes 52
  29.6 10.9 %copy-start.1 = (s32[4]{0:T(128)S(1)}, s32[4]{0:T(128)}, u32[]{:S(2)}) copy-start(s32[4]{0:T(128)} %param.14) | copy-start | bytes 52
  29.6 10.9 %copy-start.5 = (s32[4]{0:T(128)S(1)}, s32[4]{0:T(128)}, u32[]{:S(2)}) copy-start(s32[4]{0:T(128)} %param.17) | copy-start | bytes 52
  38.0 14.2 %copy-start.3 = (f32[4,128]{1,0:T(4,128)}, f32[4,128]{1,0:T(4,128)S(1)}, u32[]{:S(2)}) copy-start(f32[4,128]{1,0:T(4,128)S(1)} %psum.7) | copy-start | bytes 6148
  38.4 3.7 %collective-permute-start = (f32[4,4]{1,0:T(4,128)S(1)}, f32[4,4]{1,0:T(4,128)S(1)}, u32[]{:S(2)}, u32[]{:S(2)}) collective-permute-start(f32[4,4]{1,0:T(4,128)S(1)} %reshape.54), channel_id=1, source_target_pairs={{0,4},{4,0},{8,12},{12,8},{1,5},{5,1},{9,13},{13,9},{2,6},{6,2},{1... | collective-permute-start | bytes 200 | tf_op jit(solution)/shard_map/ppermute | solution.py:19
  42.1 4.5 %collective-permute-start.1 = (f32[4,4]{1,0:T(4,128)S(1)}, f32[4,4]{1,0:T(4,128)S(1)}, u32[]{:S(2)}, u32[]{:S(2)}) collective-permute-start(f32[4,4]{1,0:T(4,128)S(1)} %add.30), channel_id=1, source_target_pairs={{0,8},{4,12},{8,0},{12,4},{1,9},{5,13},{9,1},{13,5},{2,10},{6,14},... | collective-permute-start | bytes 200 | tf_op jit(solution)/shard_map/ppermute | solution.py:19
